TPU v7x, 32 devices: a whole 2x2x4 slice. The times are simulated.
32 devices in a mesh: groups: 2 (over y), tensor: 4 (over z), seq: 4 (over x, core).
Axes of the slice: x: 2, y: 2, z: 4, core: 2. Of those that a mesh axis runs over, the one named last changes fastest.
Arguments:
- stream: bfloat16 [2048, 4096], P(('groups', 'seq'), 'tensor'), parts along dimension 0, may hold values from -150 to 150, as said below
- ffn_gain: float32 [4096], replicated, may hold values from 0.5 to 1.5
- final_gain: float32 [4096], replicated, may hold values from 0.5 to 1.5
- w_gate: bfloat16 [4096, 5120], P(None, 'tensor'), may hold values from -0.09375 to 0.09375
- w_up: bfloat16 [4096, 5120], P(None, 'tensor'), may hold values from -0.09375 to 0.09375
- w_out: bfloat16 [5120, 4096], P('tensor'), may hold values from -0.25 to 0.25
- w_key: bfloat16 [4096, 2048], P(None, 'tensor'), may hold values from -0.09375 to 0.09375
- w_value: bfloat16 [4096, 2048], P(None, 'tensor'), may hold values from -0.09375 to 0.09375
Outputs:
- enc_out: bfloat16 [2048, 4096], P(('groups', 'seq'), 'tensor'), parts along dimension 0
- cross_keys: bfloat16 [2048, 2048], P('groups', 'tensor'), parts along dimension 0
- cross_values: bfloat16 [2048, 2048], P('groups', 'tensor'), parts along dimension 0
There are 2 independent parts, one for each index of `groups`. A program takes and returns all parts, laid end to end along the dimension named above; an argument that names none is the same for every part. Nothing has to cross between parts.
Inputs may be any that keep to these rules, and one draw needn't show every extreme that they name: Finite entries of the residual stream.
All inputs are finite; a program needn't handle non-finite values.
Results may differ from a plain program's by a relative error of at most 0.0055.
Values may be sent and summed in bfloat16 or wider, within the bound.
A program may use at most 128 MiB of HBM per device.

v0:
```python
import jax
import jax.numpy as jnp
from jax import lax
from jax.sharding import PartitionSpec as P

epsilon = 1e-06


def rms_norm(vector, gain):
    return vector * lax.rsqrt(jnp.mean(vector * vector, axis=-1, keepdims=True) + epsilon) * gain


def on_device(stream, ffn_gain, final_gain, w_gate, w_up, w_out, w_key, w_value):
    stream_full = lax.all_gather(stream, "tensor", axis=1, tiled=True)
    stream_wide = stream_full.astype(jnp.float32)
    feat_cols = stream.shape[1]
    feat_start = lax.axis_index("tensor") * feat_cols
    normed_in = rms_norm(stream_wide, ffn_gain).astype(jnp.bfloat16)
    gate_act = jnp.dot(normed_in, w_gate, preferred_element_type=jnp.float32)
    up_proj = jnp.dot(normed_in, w_up, preferred_element_type=jnp.float32)
    hidden = (jax.nn.gelu(gate_act, approximate=True) * up_proj).astype(jnp.bfloat16)
    row_share = stream.shape[0] // lax.axis_size("tensor")
    share_rows = lax.psum_scatter(
        jnp.dot(hidden, w_out, preferred_element_type=jnp.float32),
        "tensor",
        scatter_dimension=0,
        tiled=True,
    )
    own_rows = lax.dynamic_slice_in_dim(
        stream_wide, lax.axis_index("tensor") * row_share, row_share, 0
    )
    normed_part = rms_norm(own_rows + share_rows, final_gain).astype(jnp.bfloat16)
    final_norm = lax.all_gather(normed_part, "tensor", axis=0, tiled=True)
    enc_out = lax.dynamic_slice_in_dim(final_norm, feat_start, feat_cols, 1)
    key_part = jnp.dot(final_norm, w_key, preferred_element_type=jnp.float32)
    value_part = jnp.dot(final_norm, w_value, preferred_element_type=jnp.float32)
    local_kv = jnp.concatenate([key_part, value_part], axis=1).astype(jnp.bfloat16)
    gathered = lax.all_gather(local_kv, "seq", axis=0, tiled=True)
    kv_cols = w_key.shape[1]
    cross_keys = gathered[:, :kv_cols]
    cross_values = gathered[:, kv_cols:]
    return (enc_out, cross_keys, cross_values)


def solution(mesh):
    placed = (
        P(("groups", "seq"), "tensor"),
        P(),
        P(),
        P(None, "tensor"),
        P(None, "tensor"),
        P("tensor", None),
        P(None, "tensor"),
        P(None, "tensor"),
    )
    return jax.shard_map(
        on_device,
        mesh=mesh,
        in_specs=placed,
        out_specs=(P(("groups", "seq"), "tensor"), P("groups", "tensor"), P("groups", "tensor")),
        check_vma=False,
    )
```

profile of v0, /device:TPU:1, one launch (start us, length us, event | category | flops | bytes accessed | tf_op | source)
XLA Modules:
  0.0 246.7 jit_solution(645178628614334696)
XLA Ops:
  7.2 0.0 all-gather.4.cloned.1.call-start
  7.2 0.7 all-gather.4.cloned.1.call-update
  7.9 0.0 reduce-scatter.2.cloned.1.call-start
  8.0 49.2 %all-gather.4.cloned.1.call-done = bf16[256,4096]{1,0:T(8,128)(2,1)} async-done(((bf16[256,1024]{1,0:T(8,128)(2,1)}), bf16[256,4096]{1,0:T(8,128)(2,1)}) %all-gather.4.cloned.1.call-update) | async-done | bytes 2097168 | tf_op jit(solution)/shard_map/all_gather | solution.py:14
  57.1 2.2 multiply_reduce_fusion
  59.4 6.9 %fusion.8 = f32[256,1280]{1,0:T(8,128)S(1)} fusion(bf16[4096,1280]{1,0:T(8,128)(2,1)} %param.11, f32[4096]{0:T(1024)S(1)} %copy-done.5, f32[256]{0:T(256)S(1)} %add_rsqrt_fusion, bf16[256,4096]{1,0:T(8,128)(2,1)S(1)} %copy-done), kind=kOutput, calls=%fused_computation.17 | convolution fusion | flops 2688548864 | bytes 13911040 | tf_op jit(solution)/shard_map/dot_general | solution.py:19
  66.3 15.7 %fusion.9 = f32[256,4096]{1,0:T(8,128)} fusion(bf16[1280,4096]{1,0:T(8,128)(2,1)} %param.13, bf16[4096,1280]{1,0:T(8,128)(2,1)} %param.12, f32[256,1280]{1,0:T(8,128)S(1)} %fusion.8, f32[4096]{0:T(1024)S(1)} %copy-done.5, f32[256]{0:T(256)S(1)} %add_rsqrt_fusion, bf16[256,4096]{1,0:T(8,128)(2,1)S(1)} %copy-done), kind=kOutput, calls=%fused_computation.19 | convolution fusion | flops 5376180224 | bytes 28591104 | tf_op jit(solution)/shard_map/dot_general | solution.py:24
  82.1 0.0 reduce-scatter.2.cloned.1.call-update
  82.1 0.0 all-gather.6.cloned.1.call-start
  82.1 2.5 convert_element_type.13
  84.6 73.1 %reduce-scatter.2.cloned.1.call-done = f32[64,4096]{1,0:T(8,128)} async-done(((f32[256,4096]{1,0:T(8,128)}), f32[64,4096]{1,0:T(8,128)}) %reduce-scatter.2.cloned.1.call-update) | async-done | bytes 1048592 | tf_op jit(solution)/shard_map/reduce_scatter | solution.py:23
  157.7 1.8 multiply_reduce_fusion.1
  159.6 2.2 multiply_convert_fusion.1
  161.8 0.0 all-gather.6.cloned.1.call-update
  161.8 0.0 all-gather.8.cloned.1.call-start
  161.9 46.4 %all-gather.6.cloned.1.call-done = bf16[256,4096]{1,0:T(8,128)(2,1)} async-done(((bf16[64,4096]{1,0:T(8,128)(2,1)}), bf16[256,4096]{1,0:T(8,128)(2,1)}) %all-gather.6.cloned.1.call-update) | async-done | bytes 2097168 | tf_op jit(solution)/shard_map/all_gather | solution.py:33
  208.3 4.2 %convolution_convert_fusion = bf16[256,512]{1,0:T(8,128)(2,1)S(1)} fusion(bf16[256,4096]{1,0:T(8,128)(2,1)} %all-gather.6.cloned.1.call-done, bf16[4096,512]{1,0:T(8,128)(2,1)} %param.15), kind=kOutput, calls=%fused_computation.12 | convolution fusion | flops 1073872896 | bytes 6553600 | tf_op jit(solution)/shard_map/dot_general | solution.py:36
  212.5 0.4 copy-done.4
  213.0 1.3 convolution_convert_fusion.1
  214.3 0.9 pad_maximum_fusion
  215.1 0.0 all-gather.8.cloned.1.call-update
  215.1 0.8 constant_dynamic-slice_fusion
  216.0 21.2 %all-gather.8.cloned.1.call-done = bf16[1024,1024]{1,0:T(8,128)(2,1)} async-done(((bf16[256,1024]{1,0:T(8,128)(2,1)}), bf16[1024,1024]{1,0:T(8,128)(2,1)}) %all-gather.8.cloned.1.call-update) | async-done | bytes 2097168 | tf_op jit(solution)/shard_map/all_gather | solution.py:38
  237.2 3.0 %fusion.14 = (bf16[1024,512]{1,0:T(8,128)(2,1)}, bf16[1024,512]{1,0:T(8,128)(2,1)}) fusion(bf16[1024,1024]{1,0:T(8,128)(2,1)} %all-gather.8.cloned.1.call-done), kind=kLoop, calls=%fused_computation.27 | loop fusion | bytes 4194304 | tf_op jit(solution)/shard_map/slice | solution.py:41
  (13 shorter events, 0.0 us)
Async XLA Ops:
  7.2 52.2 %copy-start.5 = (f32[4096]{0:T(1024)S(1)}, f32[4096]{0:T(1024)}, u32[]{:S(2)}) copy-start(f32[4096]{0:T(1024)} %param.9) | copy-start | bytes 49156
  7.2 50.0 %all-gather.4.cloned.1.call-start = ((), (), s32[]{:S(2)}) async-start(), calls=%async_computation.1 | async-start | bytes 2621440 | tf_op jit(solution)/shard_map/all_gather | solution.py:14
  7.9 149.8 %reduce-scatter.2.cloned.1.call-start = ((), (), s32[]{:S(2)}) async-start(), calls=%async_computation.2 | async-start | bytes 5242880 | tf_op jit(solution)/shard_map/reduce_scatter | solution.py:23
  57.1 2.3 copy-start
  82.1 126.2 %all-gather.6.cloned.1.call-start = ((), (), s32[]{:S(2)}) async-start(), calls=%async_computation.3 | async-start | bytes 2621440 | tf_op jit(solution)/shard_map/all_gather | solution.py:33
  84.6 74.9 %copy-start.3 = (f32[4096]{0:T(1024)S(1)}, f32[4096]{0:T(1024)}, u32[]{:S(2)}) copy-start(f32[4096]{0:T(1024)} %param.10) | copy-start | bytes 49156
  157.7 1.9 copy-start.1
  161.8 75.4 %all-gather.8.cloned.1.call-start = ((), (), s32[]{:S(2)}) async-start(), calls=%async_computation.4 | async-start | bytes 2621440 | tf_op jit(solution)/shard_map/all_gather | solution.py:38
  208.3 4.2 %copy-start.2 = (bf16[256,4096]{1,0:T(8,128)(2,1)S(1)}, bf16[256,4096]{1,0:T(8,128)(2,1)}, u32[]{:S(2)}) copy-start(bf16[256,4096]{1,0:T(8,128)(2,1)} %all-gather.6.cloned.1.call-done) | copy-start | bytes 6291460
  208.3 4.7 %copy-start.4 = (bf16[4096,512]{1,0:T(8,128)(2,1)S(1)}, bf16[4096,512]{1,0:T(8,128)(2,1)}, u32[]{:S(2)}) copy-start(bf16[4096,512]{1,0:T(8,128)(2,1)} %param.14) | copy-start | bytes 12582916
Sparse Core Ops, SparseCore 0:
  9.6 47.5 all-gather.3
  82.2 75.4 reduce-scatter.1
  162.0 46.2 all-gather.5
  215.3 21.9 all-gather.7
where the time goes:
time: 247 us
  waiting for transfers between devices  191 us (77%)
  matrix products  28.1 us (11%)
  between operations  13.9 us (6%)
  other arithmetic  9.64 us (4%)
  local copies, waits for them, and re-layouts  4.29 us (2%)
    reduce_scatter x1, waiting for transfers between devices, on_device(): lax.psum_scatter(jnp.dot(hidden, w_out, preferred_element_type=jnp.float3...  73.1 us
    all_gather x1, waiting for transfers between devices, on_device(): stream_full = lax.all_gather(stream, 'tensor', axis=1, tiled=True)  49.2 us
    all_gather x1, waiting for transfers between devices, on_device(): final_norm = lax.all_gather(normed_part, 'tensor', axis=0, tiled=True)  46.4 us
    all_gather x1, waiting for transfers between devices, on_device(): gathered = lax.all_gather(local_kv, 'seq', axis=0, tiled=True)  21.2 us
    dot_general x1, matrix products, on_device(): jnp.dot(hidden, w_out, preferred_element_type=jnp.float32)  15.7 us
    dot_general x1, matrix products, on_device(): gate_act = jnp.dot(normed_in, w_gate, preferred_element_type=jnp.float32)  6.9 us
  transfers between devices with their start and end apart: 4, of which 4 were waited for; matrix products, arithmetic and copies ran while one was open for 1% of the time, Pallas kernels for 0%

commit v1 on v0

v1 whole, which is shorter than its diff:
```python
import functools

import jax
import jax.numpy as jnp
from jax import lax
from jax.experimental import pallas as pl
from jax.experimental.pallas import tpu as pltpu
from jax.sharding import PartitionSpec as P

epsilon = 1e-06
MESH = pl.DeviceIdType.MESH
CHUNKS = 2
SUBS = 2


def block_kernel(
    n, m,
    x_hbm, fg_ref, eg_ref, wg_hbm, wu_hbm, wo_hbm, wk_hbm, wv_hbm,
    enc_hbm, key_hbm, val_hbm,
    wg, wu, wo, wk, wv,
    xs, ms, sent, from_left, from_right,
    gate, up, hid, part, mixed, ssq, kacc, vacc, rsq, enc, kv,
    wsem, xsem, a1s, a1r, rss, rsr, a2s, a2r, sqs, sqr, kvs, kvr, osem,
):
    t = lax.axis_index("tensor")
    s = lax.axis_index("seq")
    _, rows, feat = xs.shape
    crow = rows // CHUNKS
    srow = crow // SUBS
    width = n * feat
    partner = s + 1 - 2 * lax.rem(s, 2)
    mates = [lax.rem(s + 2 * d, m) for d in range(1, m // 2)]
    peers = [lax.rem(t + d, n) for d in range(1, n)]

    def fblk(j):
        return pl.ds(pl.multiple_of(j * feat, feat), feat)

    def x_copy(c):
        r = pl.ds(c * crow, crow)
        return pltpu.make_async_copy(x_hbm.at[r], xs.at[t, r], xsem.at[c])

    def w_in(i, src, dst, j):
        return pltpu.make_async_copy(src.at[fblk(j)], dst.at[fblk(j)], wsem.at[i, j])

    wo_copy = pltpu.make_async_copy(wo_hbm, wo, wsem.at[4, 0])
    for c in range(CHUNKS):
        x_copy(c).start()

    def first_weights(d, carry):
        j = lax.rem(t + d, n)
        w_in(0, wg_hbm, wg, j).start()
        w_in(1, wu_hbm, wu, j).start()
        return carry

    def last_weights(d, carry):
        w_in(2, wk_hbm, wk, d).start()
        w_in(3, wv_hbm, wv, d).start()
        return carry

    lax.fori_loop(0, n, first_weights, 0)
    wo_copy.start()
    lax.fori_loop(0, n, last_weights, 0)

    barrier = pltpu.get_barrier_semaphore()
    for p in peers:
        pl.semaphore_signal(barrier, inc=1, device_id={"tensor": p}, device_id_type=MESH)
    for q in mates + [partner]:
        pl.semaphore_signal(barrier, inc=1, device_id={"seq": q}, device_id_type=MESH)
    pl.semaphore_wait(barrier, len(peers) + len(mates) + 1)

    def hop(buf, ssem, rsem, side, j, c, g):
        r = pl.ds(c * crow + g * srow, srow)
        to = t + 1 if side == 0 else t - 1
        return pltpu.make_async_remote_copy(
            src_ref=buf.at[j, r],
            dst_ref=buf.at[j, r],
            send_sem=ssem.at[side, j, c * SUBS + g],
            recv_sem=rsem.at[j, c * SUBS + g],
            device_id={"tensor": to},
            device_id_type=MESH,
        )

    def gather_start(buf, ssem, rsem, c):
        for g in range(SUBS):
            @pl.when(t < n - 1)
            def _():
                hop(buf, ssem, rsem, 0, t, c, g).start()

            @pl.when(t > 0)
            def _():
                hop(buf, ssem, rsem, 1, t, c, g).start()

    def gather_pass(buf, ssem, rsem, c, d):
        for g in range(SUBS):
            @pl.when(t - d >= 0)
            def _():
                j = t - d
                hop(buf, ssem, rsem, 0, j, c, g).wait_recv()

                @pl.when(t < n - 1)
                def _():
                    hop(buf, ssem, rsem, 0, j, c, g).start()

            @pl.when(t + d < n)
            def _():
                j = t + d
                hop(buf, ssem, rsem, 1, j, c, g).wait_recv()

                @pl.when(t > 0)
                def _():
                    hop(buf, ssem, rsem, 1, j, c, g).start()

    def gather_drain(buf, ssem, rsem):
        def body(j, carry):
            for c in range(CHUNKS):
                for g in range(SUBS):
                    @pl.when((t < n - 1) & (j <= t))
                    def _():
                        hop(buf, ssem, rsem, 0, j, c, g).wait_send()

                    @pl.when((t > 0) & (j >= t))
                    def _():
                        hop(buf, ssem, rsem, 1, j, c, g).wait_send()
            return carry

        lax.fori_loop(0, n, body, 0)

    def on_blocks(d, work):
        def body(i, carry):
            j = t - d + 2 * d * i

            @pl.when((j >= 0) & (j < n) & ((d > 0) | (i == 0)))
            def _():
                work(j)
            return carry

        lax.fori_loop(0, 2, body, 0)

    def project(c, j):
        if c == 0:
            w_in(0, wg_hbm, wg, j).wait()
            w_in(1, wu_hbm, wu, j).wait()
        x = xs[j, pl.ds(c * crow, crow), :].astype(jnp.float32)
        rsq[...] += jnp.sum(x * x, axis=1, keepdims=True)
        xg = (x * fg_ref[:, fblk(j)]).astype(jnp.bfloat16)
        gate[...] += jnp.dot(xg, wg[fblk(j), :], preferred_element_type=jnp.float32)
        up[...] += jnp.dot(xg, wu[fblk(j), :], preferred_element_type=jnp.float32)

    def enter_in(c):
        gate[...] = jnp.zeros_like(gate)
        up[...] = jnp.zeros_like(up)
        rsq[...] = jnp.zeros_like(rsq)
        x_copy(c).wait()
        gather_start(xs, a1s, a1r, c)

    def in_step(c, d):
        @pl.when(d > 0)
        def _():
            gather_pass(xs, a1s, a1r, c, d)
        on_blocks(d, functools.partial(project, c))

    def make_hidden():
        rstd = lax.rsqrt(rsq[...] / width + epsilon)
        hid[...] = (jax.nn.gelu(gate[...] * rstd, approximate=True) * (up[...] * rstd)).astype(jnp.bfloat16)

    def sum_hop(side, j, c, g):
        r = pl.ds(c * crow + g * srow, srow)
        dst = from_left if side == 0 else from_right
        return pltpu.make_async_remote_copy(
            src_ref=sent.at[j, r],
            dst_ref=dst.at[j, r],
            send_sem=rss.at[j, c * SUBS + g],
            recv_sem=rsr.at[side, j, c * SUBS + g],
            device_id={"tensor": t + 1 if side == 0 else t - 1},
            device_id_type=MESH,
        )

    def product(j):
        part[...] = jnp.dot(hid[...], wo[:, fblk(j)], preferred_element_type=jnp.float32)

    def sum_send(side, j, c):
        arrives = (t > 0) if side == 0 else (t < n - 1)
        buf = from_left if side == 0 else from_right
        for g in range(SUBS):
            r = pl.ds(c * crow + g * srow, srow)
            pr = pl.ds(g * srow, srow)

            @pl.when(arrives)
            def _():
                sum_hop(side, j, c, g).wait_recv()
                sent[j, r, :] = (part[pr, :] + buf[j, r, :].astype(jnp.float32)).astype(jnp.bfloat16)

            @pl.when(jnp.logical_not(arrives))
            def _():
                sent[j, r, :] = part[pr, :].astype(jnp.bfloat16)
            sum_hop(side, j, c, g).start()

    def sum_step(c, d):
        @pl.when(d >= t)
        def _():
            j = n - 1 - (d - t)
            product(j)
            sum_send(0, j, c)

        @pl.when(d >= n - 1 - t)
        def _():
            j = d - (n - 1 - t)
            product(j)
            sum_send(1, j, c)

    def sum_own(c):
        r = pl.ds(c * crow, crow)
        product(t)
        part[...] += xs[t, r, :].astype(jnp.float32)

        @pl.when(t > 0)
        def _():
            for g in range(SUBS):
                sum_hop(0, t, c, g).wait_recv()
            part[...] += from_left[t, r, :].astype(jnp.float32)

        @pl.when(t < n - 1)
        def _():
            for g in range(SUBS):
                sum_hop(1, t, c, g).wait_recv()
            part[...] += from_right[t, r, :].astype(jnp.float32)
        mix = part[...]
        scaled = mix * eg_ref[:, fblk(t)]
        ms[t, r, :] = scaled.astype(jnp.bfloat16)
        mixed[c] = scaled
        gather_start(ms, a2s, a2r, c)
        total = jnp.sum(mix * mix, axis=1, keepdims=True)
        ssq[c, t] = jnp.transpose(jnp.broadcast_to(total, (crow, 128)), (1, 0))[:8]
        for p in peers:
            sq_copy(c, t, p).start()

    def sq_copy(c, j, p):
        return pltpu.make_async_remote_copy(
            src_ref=ssq.at[c, j],
            dst_ref=ssq.at[c, j],
            send_sem=sqs.at[c, p],
            recv_sem=sqr.at[c, j],
            device_id={"tensor": p},
            device_id_type=MESH,
        )

    def key_value(c, j):
        if c == 0:
            w_in(2, wk_hbm, wk, j).wait()
            w_in(3, wv_hbm, wv, j).wait()
        y = ms[j, pl.ds(c * crow, crow), :]
        kacc[...] += jnp.dot(y, wk[fblk(j), :], preferred_element_type=jnp.float32)
        vacc[...] += jnp.dot(y, wv[fblk(j), :], preferred_element_type=jnp.float32)

    def out_step(c, d):
        @pl.when(d > 0)
        def _():
            gather_pass(ms, a2s, a2r, c, d)
        on_blocks(d, functools.partial(key_value, c))

    def enter_out():
        kacc[...] = jnp.zeros_like(kacc)
        vacc[...] = jnp.zeros_like(vacc)

    def kv_copy(c, owner, slot, to):
        return pltpu.make_async_remote_copy(
            src_ref=kv.at[owner, c],
            dst_ref=kv.at[owner, c],
            send_sem=kvs.at[slot, c],
            recv_sem=kvr.at[owner, c],
            device_id={"seq": to},
            device_id_type=MESH,
        )

    def store_kv(c, owner, slot):
        r = pl.ds(pl.multiple_of(owner * rows + c * crow, crow), crow)
        return (
            pltpu.make_async_copy(kv.at[owner, c, 0], key_hbm.at[r], osem.at[0, slot, c]),
            pltpu.make_async_copy(kv.at[owner, c, 1], val_hbm.at[r], osem.at[1, slot, c]),
        )

    def enc_store(c):
        r = pl.ds(c * crow, crow)
        return pltpu.make_async_copy(enc.at[r], enc_hbm.at[r], osem.at[0, m, c])

    def finish(c):
        total = ssq[c, t]
        for p in peers:
            sq_copy(c, p, p).wait_recv()
            total = total + ssq[c, p]
        column = jnp.transpose(jnp.broadcast_to(total[:1], (128, crow)), (1, 0))[:, :1]
        rstd = lax.rsqrt(column / width + epsilon)
        kv[s, c, 0] = (kacc[...] * rstd).astype(jnp.bfloat16)
        kv[s, c, 1] = (vacc[...] * rstd).astype(jnp.bfloat16)
        for i, q in enumerate(mates):
            kv_copy(c, s, i, q).start()
        kv_copy(c, s, m - 1, partner).start()
        enc[pl.ds(c * crow, crow), :] = (mixed[c] * rstd).astype(jnp.bfloat16)
        enc_store(c).start()
        for cp in store_kv(c, s, 0):
            cp.start()

    def pass_kv(c):
        for i, q in enumerate(mates):
            kv_copy(c, q, i, q).wait_recv()
            kv_copy(c, q, len(mates) + i, partner).start()
            for cp in store_kv(c, q, 1 + i):
                cp.start()

    def take_kv(c):
        for i in range(m // 2):
            q = lax.rem(partner + 2 * i, m)
            kv_copy(c, q, m - 1, partner).wait_recv()
            for cp in store_kv(c, q, m // 2 + i):
                cp.start()

    def steps(lo, hi, *works):
        def body(d, carry):
            for w in works:
                w(d)
            return carry

        lax.fori_loop(lo, hi, body, 0)

    def at(f, c):
        return functools.partial(f, c)

    last = n - 1
    enter_in(0)
    steps(0, n, at(in_step, 0))
    make_hidden()
    wo_copy.wait()
    for c in range(CHUNKS):
        more = c + 1 < CHUNKS
        before = c > 0
        if more:
            enter_in(c + 1)
        if before:
            enter_out()
        works = []
        if more:
            works.append(at(in_step, c + 1))
        if before:
            works.append(at(out_step, c - 1))
        steps(0, last, *(works + [at(sum_step, c)]))
        for w in works:
            w(jnp.int32(last))
        sum_own(c)
        if before:
            finish(c - 1)
        if more:
            make_hidden()
    c = CHUNKS - 1
    enter_out()
    steps(0, n, at(out_step, c))
    finish(c)
    for b in range(CHUNKS):
        pass_kv(b)
    for b in range(CHUNKS):
        take_kv(b)

    gather_drain(xs, a1s, a1r)
    gather_drain(ms, a2s, a2r)

    def sums_drain(j, carry):
        for c in range(CHUNKS):
            for g in range(SUBS):
                @pl.when(j > t)
                def _():
                    sum_hop(0, j, c, g).wait_send()

                @pl.when(j < t)
                def _():
                    sum_hop(1, j, c, g).wait_send()
        return carry

    lax.fori_loop(0, n, sums_drain, 0)
    for c in range(CHUNKS):
        for p in peers:
            sq_copy(c, t, p).wait_send()
        for i, q in enumerate(mates):
            kv_copy(c, s, i, q).wait_send()
            kv_copy(c, q, len(mates) + i, partner).wait_send()
        kv_copy(c, s, m - 1, partner).wait_send()
        enc_store(c).wait()
        for slot in range(m):
            for cp in store_kv(c, s, slot):
                cp.wait()


def on_device(n, m, stream, ffn_gain, final_gain, w_gate, w_up, w_out, w_key, w_value):
    rows, feat = stream.shape
    width = n * feat
    ffc = w_gate.shape[1]
    kvc = w_key.shape[1]
    crow = rows // CHUNKS
    bf, f32 = jnp.bfloat16, jnp.float32
    dma = pltpu.SemaphoreType.DMA
    any_spec = pl.BlockSpec(memory_space=pl.ANY)
    vmem = pl.BlockSpec(memory_space=pltpu.VMEM)
    parts = CHUNKS * SUBS
    return pl.pallas_call(
        functools.partial(block_kernel, n, m),
        out_shape=(
            jax.ShapeDtypeStruct((rows, feat), bf),
            jax.ShapeDtypeStruct((m * rows, kvc), bf),
            jax.ShapeDtypeStruct((m * rows, kvc), bf),
        ),
        in_specs=[any_spec, vmem, vmem] + [any_spec] * 5,
        out_specs=(any_spec,) * 3,
        scratch_shapes=[
            pltpu.VMEM((width, ffc), bf),
            pltpu.VMEM((width, ffc), bf),
            pltpu.VMEM((ffc, width), bf),
            pltpu.VMEM((width, kvc), bf),
            pltpu.VMEM((width, kvc), bf),
            pltpu.VMEM((n, rows, feat), bf),
            pltpu.VMEM((n, rows, feat), bf),
            pltpu.VMEM((n, rows, feat), bf),
            pltpu.VMEM((n, rows, feat), bf),
            pltpu.VMEM((n, rows, feat), bf),
            pltpu.VMEM((crow, ffc), f32),
            pltpu.VMEM((crow, ffc), f32),
            pltpu.VMEM((crow, ffc), bf),
            pltpu.VMEM((crow, feat), f32),
            pltpu.VMEM((CHUNKS, crow, feat), f32),
            pltpu.VMEM((CHUNKS, n, 8, crow), f32),
            pltpu.VMEM((crow, kvc), f32),
            pltpu.VMEM((crow, kvc), f32),
            pltpu.VMEM((crow, 1), f32),
            pltpu.VMEM((rows, feat), bf),
            pltpu.VMEM((m, CHUNKS, 2, crow, kvc), bf),
            dma((5, n)),
            dma((CHUNKS,)),
            dma((2, n, parts)),
            dma((n, parts)),
            dma((n, parts)),
            dma((2, n, parts)),
            dma((2, n, parts)),
            dma((n, parts)),
            dma((CHUNKS, n)),
            dma((CHUNKS, n)),
            dma((m, CHUNKS)),
            dma((m, CHUNKS)),
            dma((2, m + 1, CHUNKS)),
        ],
        compiler_params=pltpu.CompilerParams(
            collective_id=0, has_side_effects=True, vmem_limit_bytes=67000000
        ),
    )(
        stream,
        ffn_gain.reshape(1, width),
        final_gain.reshape(1, width),
        w_gate, w_up, w_out, w_key, w_value,
    )


def solution(mesh):
    placed = (
        P(("groups", "seq"), "tensor"),
        P(),
        P(),
        P(None, "tensor"),
        P(None, "tensor"),
        P("tensor", None),
        P(None, "tensor"),
        P(None, "tensor"),
    )
    return jax.shard_map(
        functools.partial(on_device, mesh.shape["tensor"], mesh.shape["seq"]),
        mesh=mesh,
        in_specs=placed,
        out_specs=(P(("groups", "seq"), "tensor"), P("groups", "tensor"), P("groups", "tensor")),
        check_vma=False,
    )
```

time: 247 us -> 110 us (0.45)
  waiting for transfers between devices: 191 us -> 0 us
  Pallas kernels: 0 us -> 102 us
  matrix products: 28.1 us -> 0 us
  between operations: 13.9 us -> 0.64 us
  other arithmetic: 9.64 us -> 0 us
    all_gather x3 -> x0, waiting for transfers between devices: 117 us -> none  [the longest x1 49.2 us: on_device(): stream_full = lax.all_gather(stream, 'tensor', axis=1, tiled=True)]
    pallas_call x0 -> x1, Pallas kernels: none -> 102 us  [on_device(): pl.pallas_call(functools.partial(block_kernel, n, m), out_shape=(jax.Shap...]
    reduce_scatter x1 -> x0, waiting for transfers between devices: 73.1 us -> none  [on_device(): lax.psum_scatter(jnp.dot(hidden, w_out, preferred_element_type=jnp.float3...]
    dot_general x4 -> x0, matrix products: 28.1 us -> none  [the longest x1 15.7 us: on_device(): jnp.dot(hidden, w_out, preferred_element_type=jnp.float32)]
    unnamed x12 -> x3, local copies, waits for them, and re-layouts: 0.45 us -> 6.39 us
    convert_element_type x2 -> x0, other arithmetic: 4.71 us -> none  [the longest x1 2.46 us: on_device(): stream_wide = stream_full.astype(jnp.float32)]
    reduce_sum x2 -> x0, other arithmetic: 4.07 us -> none  [rms_norm(): jnp.mean(vector * vector, axis=-1, keepdims=True) + epsilon]
    slice x1 -> x0, local copies, waits for them, and re-layouts: 2.99 us -> none  [on_device(): cross_values = gathered[:, kv_cols:]]
  transfers between devices with their start and end apart: 4 -> 0, of which waited for: 4 -> 0; matrix products, arithmetic and copies ran while one was open for 1% -> 0% of each run, Pallas kernels for 0% -> 0%
where the time goes in v1:
time: 110 us; the launch traced here: 109 us
  Pallas kernels  102 us (93%)
  local copies, waits for them, and re-layouts  6.39 us (6%)
    pallas_call x1, Pallas kernels, on_device(): pl.pallas_call(functools.partial(block_kernel, n, m), out_shape=(jax.Shap...  102 us
    unnamed x3, local copies, waits for them, and re-layouts  6.39 us

profile of v1, /device:TPU:1, one launch (start us, length us, event | category | flops | bytes accessed | tf_op | source)
XLA Modules:
  0.0 109.5 jit_solution(11044838458681996450)
XLA Ops:
  0.6 102.4 %shard_map.103 = (bf16[256,1024]{1,0:T(8,128)(2,1)}, bf16[1024,512]{1,0:T(8,128)(2,1)}, bf16[1024,512]{1,0:T(8,128)(2,1)}) custom-call(bf16[256,1024]{1,0:T(8,128)(2,1)} %x_hbm.1, f32[1,4096]{1,0:T(1,128)} %bitcast.2, f32[1,4096]{1,0:T(1,128)} %bitcast.3, bf16[4096,1280]{1,0:T(8,128)(2,1)} %wg_hbm.1, bf16[4096,1280]{1,0:T(8,128)(2,1)} %wu_hbm.1, ...), custom_call_target="tpu_custom_call" | custom-call | tf_op jit(solution)/shard_map/pallas_call | solution.py:402
  103.1 1.9 %copy.14 = bf16[256,1024]{1,0:T(8,128)(2,1)} copy(bf16[256,1024]{1,0:T(8,128)(2,1)} %get-tuple-element.6) | data formatting | bytes 1048576
  105.0 2.3 %copy.15 = bf16[1024,512]{1,0:T(8,128)(2,1)} copy(bf16[1024,512]{1,0:T(8,128)(2,1)} %get-tuple-element.7) | data formatting | bytes 2097152
  107.2 2.3 %copy.16 = bf16[1024,512]{1,0:T(8,128)(2,1)} copy(bf16[1024,512]{1,0:T(8,128)(2,1)} %get-tuple-element.8) | data formatting | bytes 2097152

commit v2 on v1

--- a/solution.py
+++ b/solution.py
@@ -80,13 +80,13 @@
             device_id_type=MESH,
         )
 
-    def gather_start(buf, ssem, rsem, c):
+    def gather_start(buf, ssem, rsem, c, up_too=True, down_too=True):
         for g in range(SUBS):
-            @pl.when(t < n - 1)
+            @pl.when((t < n - 1) & up_too)
             def _():
                 hop(buf, ssem, rsem, 0, t, c, g).start()
 
-            @pl.when(t > 0)
+            @pl.when((t > 0) & down_too)
             def _():
                 hop(buf, ssem, rsem, 1, t, c, g).start()
 
@@ -150,13 +150,13 @@
         gate[...] = jnp.zeros_like(gate)
         up[...] = jnp.zeros_like(up)
         rsq[...] = jnp.zeros_like(rsq)
-        x_copy(c).wait()
-        gather_start(xs, a1s, a1r, c)
 
     def in_step(c, d):
         @pl.when(d > 0)
         def _():
             gather_pass(xs, a1s, a1r, c, d)
+        if c + 1 < CHUNKS:
+            gather_start(xs, a1s, a1r, c + 1, d == t, d == n - 1 - t)
         on_blocks(d, functools.partial(project, c))
 
     def make_hidden():
@@ -326,6 +326,9 @@
         return functools.partial(f, c)
 
     last = n - 1
+    for c in range(CHUNKS):
+        x_copy(c).wait()
+    gather_start(xs, a1s, a1r, 0)
     enter_in(0)
     steps(0, n, at(in_step, 0))
     make_hidden()
@@ -388,6 +391,39 @@
                 cp.wait()
 
 
+def write_kernel(pieces, *refs):
+    count = (len(refs) - 2) // 3
+    srcs, dsts, bufs = refs[:count], refs[count:2 * count], refs[2 * count:3 * count]
+    isem, wsem = refs[3 * count:]
+    loads, stores = [], []
+    for i in range(count):
+        size = srcs[i].shape[0] // pieces
+        for k in range(pieces):
+            r = pl.ds(k * size, size)
+            loads.append(pltpu.make_async_copy(srcs[i].at[r], bufs[i].at[r], isem.at[i, k]))
+            stores.append(pltpu.make_async_copy(bufs[i].at[r], dsts[i].at[r], wsem.at[i, k]))
+    for load in loads:
+        load.start()
+    for load, store in zip(loads, stores):
+        load.wait()
+        store.start()
+    for store in stores:
+        store.wait()
+
+
+def write_out(arrays):
+    count, pieces = len(arrays), 2
+    any_spec = pl.BlockSpec(memory_space=pl.ANY)
+    return pl.pallas_call(
+        functools.partial(write_kernel, pieces),
+        out_shape=tuple(jax.ShapeDtypeStruct(a.shape, a.dtype) for a in arrays),
+        in_specs=[any_spec] * count,
+        out_specs=(any_spec,) * count,
+        scratch_shapes=[pltpu.VMEM(a.shape, a.dtype) for a in arrays]
+        + [pltpu.SemaphoreType.DMA((count, pieces))] * 2,
+    )(*arrays)
+
+
 def on_device(n, m, stream, ffn_gain, final_gain, w_gate, w_up, w_out, w_key, w_value):
     rows, feat = stream.shape
     width = n * feat
@@ -399,7 +435,7 @@
     any_spec = pl.BlockSpec(memory_space=pl.ANY)
     vmem = pl.BlockSpec(memory_space=pltpu.VMEM)
     parts = CHUNKS * SUBS
-    return pl.pallas_call(
+    made = pl.pallas_call(
         functools.partial(block_kernel, n, m),
         out_shape=(
             jax.ShapeDtypeStruct((rows, feat), bf),
@@ -453,6 +489,7 @@
         final_gain.reshape(1, width),
         w_gate, w_up, w_out, w_key, w_value,
     )
+    return write_out(made)
 
 
 def solution(mesh):

time: 110 us -> 101 us (0.918)
  local copies, waits for them, and re-layouts: 6.39 us -> 0 us
  Pallas kernels: 102 us -> 100 us
    unnamed x3 -> x0, local copies, waits for them, and re-layouts: 6.39 us -> none
    pallas_call x1, Pallas kernels: 102 us -> 97.9 us  [on_device(): pl.pallas_call(functools.partial(block_kernel, n, m), out_shape=(jax.Shap...]
    pallas_call x0 -> x1, Pallas kernels: none -> 2.62 us  [write_out(): pl.pallas_call(functools.partial(write_kernel, pieces), out_shape=tuple((...]
where the time goes in v2:
time: 101 us
  Pallas kernels  100 us (99%)
    pallas_call x1, Pallas kernels, on_device(): pl.pallas_call(functools.partial(block_kernel, n, m), out_shape=(jax.Shap...  97.9 us
    pallas_call x1, Pallas kernels, write_out(): pl.pallas_call(functools.partial(write_kernel, pieces), out_shape=tuple((...  2.62 us

profile of v2, /device:TPU:1, one launch (start us, length us, event | category | flops | bytes accessed | tf_op | source)
XLA Modules:
  0.0 101.1 jit_solution(12804849640777094142)
XLA Ops:
  0.6 97.9 %shard_map.103 = (bf16[256,1024]{1,0:T(8,128)(2,1)}, bf16[1024,512]{1,0:T(8,128)(2,1)}, bf16[1024,512]{1,0:T(8,128)(2,1)}) custom-call(bf16[256,1024]{1,0:T(8,128)(2,1)} %x_hbm.1, f32[1,4096]{1,0:T(1,128)} %bitcast.2, f32[1,4096]{1,0:T(1,128)} %bitcast.3, bf16[4096,1280]{1,0:T(8,128)(2,1)} %wg_hbm.1, bf16[4096,1280]{1,0:T(8,128)(2,1)} %wu_hbm.1, ...), custom_call_target="tpu_custom_call" | custom-call | tf_op jit(solution)/shard_map/pallas_call | solution.py:438
  98.5 2.6 %shard_map.104 = (bf16[256,1024]{1,0:T(8,128)(2,1)}, bf16[1024,512]{1,0:T(8,128)(2,1)}, bf16[1024,512]{1,0:T(8,128)(2,1)}) custom-call(bf16[256,1024]{1,0:T(8,128)(2,1)} %get-tuple-element.6.refs_0_, bf16[1024,512]{1,0:T(8,128)(2,1)} %get-tuple-element.7.refs_1_, bf16[1024,512]{1,0:T(8,128)(2,1)} %get-tuple-element.8.refs_2_), custom_call_target="tpu_custom_call" | custom-call | tf_op jit(solution)/shard_map/pallas_call | solution.py:417

commit v3 on v2

--- a/solution.py
+++ b/solution.py
@@ -19,7 +19,7 @@
     enc_hbm, key_hbm, val_hbm,
     wg, wu, wo, wk, wv,
     xs, ms, sent, from_left, from_right,
-    gate, up, hid, part, mixed, ssq, kacc, vacc, rsq, enc, kv,
+    gate, up, hid, part, mixed, ssq, kacc, vacc, rsq, rsq2, enc, kv,
     wsem, xsem, a1s, a1r, rss, rsr, a2s, a2r, sqs, sqr, kvs, kvr, osem,
 ):
     t = lax.axis_index("tensor")
@@ -90,8 +90,8 @@
             def _():
                 hop(buf, ssem, rsem, 1, t, c, g).start()
 
-    def gather_pass(buf, ssem, rsem, c, d):
-        for g in range(SUBS):
+    def gather_pass(buf, ssem, rsem, c, d, subs=range(SUBS)):
+        for g in subs:
             @pl.when(t - d >= 0)
             def _():
                 j = t - d
@@ -248,9 +248,13 @@
         if c == 0:
             w_in(2, wk_hbm, wk, j).wait()
             w_in(3, wv_hbm, wv, j).wait()
-        y = ms[j, pl.ds(c * crow, crow), :]
-        kacc[...] += jnp.dot(y, wk[fblk(j), :], preferred_element_type=jnp.float32)
-        vacc[...] += jnp.dot(y, wv[fblk(j), :], preferred_element_type=jnp.float32)
+        key_value_rows(c, 0, crow, j)
+
+    def key_value_rows(c, at_row, count, j):
+        y = ms[j, pl.ds(c * crow + at_row, count), :]
+        pr = pl.ds(at_row, count)
+        kacc[pr, :] += jnp.dot(y, wk[fblk(j), :], preferred_element_type=jnp.float32)
+        vacc[pr, :] += jnp.dot(y, wv[fblk(j), :], preferred_element_type=jnp.float32)
 
     def out_step(c, d):
         @pl.when(d > 0)
@@ -262,56 +266,61 @@
         kacc[...] = jnp.zeros_like(kacc)
         vacc[...] = jnp.zeros_like(vacc)
 
-    def kv_copy(c, owner, slot, to):
+    def kv_copy(k, owner, slot, to):
         return pltpu.make_async_remote_copy(
-            src_ref=kv.at[owner, c],
-            dst_ref=kv.at[owner, c],
-            send_sem=kvs.at[slot, c],
-            recv_sem=kvr.at[owner, c],
+            src_ref=kv.at[owner, k],
+            dst_ref=kv.at[owner, k],
+            send_sem=kvs.at[slot, k],
+            recv_sem=kvr.at[owner, k],
             device_id={"seq": to},
             device_id_type=MESH,
         )
 
-    def store_kv(c, owner, slot):
-        r = pl.ds(pl.multiple_of(owner * rows + c * crow, crow), crow)
+    def store_kv(k, owner, slot):
+        r = pl.ds(pl.multiple_of(owner * rows + k * srow, srow), srow)
         return (
-            pltpu.make_async_copy(kv.at[owner, c, 0], key_hbm.at[r], osem.at[0, slot, c]),
-            pltpu.make_async_copy(kv.at[owner, c, 1], val_hbm.at[r], osem.at[1, slot, c]),
+            pltpu.make_async_copy(kv.at[owner, k, 0], key_hbm.at[r], osem.at[0, slot, k]),
+            pltpu.make_async_copy(kv.at[owner, k, 1], val_hbm.at[r], osem.at[1, slot, k]),
         )
 
-    def enc_store(c):
-        r = pl.ds(c * crow, crow)
-        return pltpu.make_async_copy(enc.at[r], enc_hbm.at[r], osem.at[0, m, c])
-
-    def finish(c):
+    def enc_store(k):
+        r = pl.ds(k * srow, srow)
+        return pltpu.make_async_copy(enc.at[r], enc_hbm.at[r], osem.at[0, m, k])
+
+    def final_scale(c):
         total = ssq[c, t]
         for p in peers:
             sq_copy(c, p, p).wait_recv()
             total = total + ssq[c, p]
         column = jnp.transpose(jnp.broadcast_to(total[:1], (128, crow)), (1, 0))[:, :1]
-        rstd = lax.rsqrt(column / width + epsilon)
-        kv[s, c, 0] = (kacc[...] * rstd).astype(jnp.bfloat16)
-        kv[s, c, 1] = (vacc[...] * rstd).astype(jnp.bfloat16)
+        rsq2[...] = lax.rsqrt(column / width + epsilon)
+
+    def finish(c, g):
+        k = c * SUBS + g
+        pr = pl.ds(g * srow, srow)
+        rstd = rsq2[pr, :]
+        kv[s, k, 0] = (kacc[pr, :] * rstd).astype(jnp.bfloat16)
+        kv[s, k, 1] = (vacc[pr, :] * rstd).astype(jnp.bfloat16)
         for i, q in enumerate(mates):
-            kv_copy(c, s, i, q).start()
-        kv_copy(c, s, m - 1, partner).start()
-        enc[pl.ds(c * crow, crow), :] = (mixed[c] * rstd).astype(jnp.bfloat16)
-        enc_store(c).start()
-        for cp in store_kv(c, s, 0):
+            kv_copy(k, s, i, q).start()
+        kv_copy(k, s, m - 1, partner).start()
+        enc[pl.ds(k * srow, srow), :] = (mixed[c, pr] * rstd).astype(jnp.bfloat16)
+        enc_store(k).start()
+        for cp in store_kv(k, s, 0):
             cp.start()
 
-    def pass_kv(c):
+    def pass_kv(k):
         for i, q in enumerate(mates):
-            kv_copy(c, q, i, q).wait_recv()
-            kv_copy(c, q, len(mates) + i, partner).start()
-            for cp in store_kv(c, q, 1 + i):
+            kv_copy(k, q, i, q).wait_recv()
+            kv_copy(k, q, len(mates) + i, partner).start()
+            for cp in store_kv(k, q, 1 + i):
                 cp.start()
 
-    def take_kv(c):
+    def take_kv(k):
         for i in range(m // 2):
             q = lax.rem(partner + 2 * i, m)
-            kv_copy(c, q, m - 1, partner).wait_recv()
-            for cp in store_kv(c, q, m // 2 + i):
+            kv_copy(k, q, m - 1, partner).wait_recv()
+            for cp in store_kv(k, q, m // 2 + i):
                 cp.start()
 
     def steps(lo, hi, *works):
@@ -350,17 +359,29 @@
             w(jnp.int32(last))
         sum_own(c)
         if before:
-            finish(c - 1)
+            final_scale(c - 1)
+            for g in range(SUBS):
+                finish(c - 1, g)
         if more:
             make_hidden()
     c = CHUNKS - 1
     enter_out()
-    steps(0, n, at(out_step, c))
-    finish(c)
-    for b in range(CHUNKS):
-        pass_kv(b)
-    for b in range(CHUNKS):
-        take_kv(b)
+    steps(0, last, at(out_step, c))
+    early = range((CHUNKS - 1) * SUBS)
+    late = range((CHUNKS - 1) * SUBS, CHUNKS * SUBS)
+    for k in early:
+        pass_kv(k)
+    final_scale(c)
+    for g in range(SUBS):
+        gather_pass(ms, a2s, a2r, c, last, (g,))
+        on_blocks(jnp.int32(last), functools.partial(key_value_rows, c, g * srow, srow))
+        finish(c, g)
+    for k in early:
+        take_kv(k)
+    for k in late:
+        pass_kv(k)
+    for k in late:
+        take_kv(k)
 
     gather_drain(xs, a1s, a1r)
     gather_drain(ms, a2s, a2r)
@@ -381,13 +402,14 @@
     for c in range(CHUNKS):
         for p in peers:
             sq_copy(c, t, p).wait_send()
+    for k in range(CHUNKS * SUBS):
         for i, q in enumerate(mates):
-            kv_copy(c, s, i, q).wait_send()
-            kv_copy(c, q, len(mates) + i, partner).wait_send()
-        kv_copy(c, s, m - 1, partner).wait_send()
-        enc_store(c).wait()
+            kv_copy(k, s, i, q).wait_send()
+            kv_copy(k, q, len(mates) + i, partner).wait_send()
+        kv_copy(k, s, m - 1, partner).wait_send()
+        enc_store(k).wait()
         for slot in range(m):
-            for cp in store_kv(c, s, slot):
+            for cp in store_kv(k, s, slot):
                 cp.wait()
 
 
@@ -464,8 +486,9 @@
             pltpu.VMEM((crow, kvc), f32),
             pltpu.VMEM((crow, kvc), f32),
             pltpu.VMEM((crow, 1), f32),
+            pltpu.VMEM((crow, 1), f32),
             pltpu.VMEM((rows, feat), bf),
-            pltpu.VMEM((m, CHUNKS, 2, crow, kvc), bf),
+            pltpu.VMEM((m, parts, 2, crow // SUBS, kvc), bf),
             dma((5, n)),
             dma((CHUNKS,)),
             dma((2, n, parts)),
@@ -476,9 +499,9 @@
             dma((n, parts)),
             dma((CHUNKS, n)),
             dma((CHUNKS, n)),
-            dma((m, CHUNKS)),
-            dma((m, CHUNKS)),
-            dma((2, m + 1, CHUNKS)),
+            dma((m, parts)),
+            dma((m, parts)),
+            dma((2, m + 1, parts)),
         ],
         compiler_params=pltpu.CompilerParams(
             collective_id=0, has_side_effects=True, vmem_limit_bytes=67000000

time: 101 us -> 100 us (0.990)
    pallas_call x1, Pallas kernels: 97.9 us -> 96.5 us  [on_device(): pl.pallas_call(functools.partial(block_kernel, n, m), out_shape=(jax.Shap...]
where the time goes in v3:
time: 100 us; the launch traced here: 99.7 us
  Pallas kernels  99.1 us (99%)
    pallas_call x1, Pallas kernels, on_device(): pl.pallas_call(functools.partial(block_kernel, n, m), out_shape=(jax.Shap...  96.5 us
    pallas_call x1, Pallas kernels, write_out(): pl.pallas_call(functools.partial(write_kernel, pieces), out_shape=tuple((...  2.62 us

profile of v3, /device:TPU:1, one launch (start us, length us, event | category | flops | bytes accessed | tf_op | source)
XLA Modules:
  0.0 99.7 jit_solution(9336013243206446336)
XLA Ops:
  0.6 96.5 %shard_map.103 = (bf16[256,1024]{1,0:T(8,128)(2,1)}, bf16[1024,512]{1,0:T(8,128)(2,1)}, bf16[1024,512]{1,0:T(8,128)(2,1)}) custom-call(bf16[256,1024]{1,0:T(8,128)(2,1)} %x_hbm.1, f32[1,4096]{1,0:T(1,128)} %bitcast.2, f32[1,4096]{1,0:T(1,128)} %bitcast.3, bf16[4096,1280]{1,0:T(8,128)(2,1)} %wg_hbm.1, bf16[4096,1280]{1,0:T(8,128)(2,1)} %wu_hbm.1, ...), custom_call_target="tpu_custom_call" | custom-call | tf_op jit(solution)/shard_map/pallas_call | solution.py:460
  97.1 2.6 %shard_map.104 = (bf16[256,1024]{1,0:T(8,128)(2,1)}, bf16[1024,512]{1,0:T(8,128)(2,1)}, bf16[1024,512]{1,0:T(8,128)(2,1)}) custom-call(bf16[256,1024]{1,0:T(8,128)(2,1)} %get-tuple-element.6.refs_0_, bf16[1024,512]{1,0:T(8,128)(2,1)} %get-tuple-element.7.refs_1_, bf16[1024,512]{1,0:T(8,128)(2,1)} %get-tuple-element.8.refs_2_), custom_call_target="tpu_custom_call" | custom-call | tf_op jit(solution)/shard_map/pallas_call | solution.py:439
